TPU v7x, 128 devices: a whole 4x4x4 slice. The times are simulated.
128 devices in a mesh: dom: 32 (over z, y, core), col: 2 (over x_hi), batch: 2 (over x_lo).
Axes of the slice: x: 4 (x_hi: 2, x_lo: 2; x = x_hi * 2 + x_lo), y: 4, z: 4, core: 2. Of those that a mesh axis runs over, the one named last changes fastest.
Arguments:
- features: bfloat16 [65536, 128], P('dom', 'col'), may hold values from -6 to 6
- self_weight1: bfloat16 [128, 256], P('col', 'batch'), may hold values from -0.5 to 0.5
- neigh_weight1: bfloat16 [128, 256], P('col', 'batch'), may hold values from -2 to 2
- need_first: int32 [64, 64], P(('dom', 'batch')), may hold values from 0 to 511, as said below
- count_first: int32 [64], P(('dom', 'batch')), may hold values from 0 to 64
- adjacency_first: int32 [65536, 512], P(('dom', 'batch')), may hold values from 0 to 16384, as said below
- self_weight2: bfloat16 [256, 172], P('col', 'batch'), may hold values from -0.375 to 0.375
- neigh_weight2: bfloat16 [256, 172], P('col', 'batch'), may hold values from -0.375 to 0.375
- need_second: int32 [64, 64], P(('dom', 'batch')), may hold values from 0 to 511, as said below
- count_second: int32 [64], P(('dom', 'batch')), may hold values from 0 to 64
- adjacency_second: int32 [65536, 512], P(('dom', 'batch')), may hold values from 0 to 16384, as said below
- seed_rows: int32 [65536], P(('dom', 'batch')), may hold values from 0 to 2047
Outputs:
- logits: float32 [65536, 172], P(('dom', 'batch'))
Inputs may be any that keep to these rules, and one draw needn't show every extreme that they name: `need_first`: each row lists 64 different node blocks in increasing order; block g holds nodes 128 * g to 128 * g + 127 and lies in partition g // 16. At most 4 entries of one row lie in one partition, and exactly 4 lie in some partition in every row. `need_second`: each row lists 64 different frontier blocks in increasing order; block g holds frontier rows 128 * g to 128 * g + 127 and lies in partition g // 16. At most 4 entries of one row lie in one partition, and exactly 4 lie in some partition in every row. `adjacency_first`: bit i of word k of a row is the adjacency entry of column 16 k + i; at most one bit of a word is set, and bit 15 never. `adjacency_second`: bit i of word k of a row is the adjacency entry of column 16 k + i; at most one bit of a word is set, and bit 15 never.
All inputs are finite; a program needn't handle non-finite values.
Results may differ from a plain program's by a relative error of at most 0.0036.
Values may be sent and summed in bfloat16 or wider, within the bound.
A program may use at most 128 MiB of HBM per device.

v0:
```python
import math
import jax
import jax.numpy as jnp
from jax import lax
from jax.sharding import PartitionSpec as P

BLK = 128


def in_blocks(shard, dim, devices):
    shape = shard.shape
    blocks = shard.reshape(*shape[:dim], devices, shape[dim] // devices, *shape[dim + 1 :])
    return jnp.moveaxis(blocks, dim, 0)


def sent_and_summed(shard, axis, dim):
    devices = lax.axis_size(axis)
    blocks = lax.all_to_all(in_blocks(shard, dim, devices), axis, 0, 0, tiled=True)
    return jnp.sum(blocks, axis=0)


def from_everyone(shard, axis):
    copies = jnp.broadcast_to(shard, (lax.axis_size(axis), *shard.shape))
    return lax.all_to_all(copies, axis, split_axis=0, concat_axis=0, tiled=True)


def of_everyone(shard, axis):
    return from_everyone(shard, axis).sum(axis=0)


def unpack_rows(packed_rows, valid_cols):
    shifts = jnp.arange(16, dtype=jnp.int32)
    bit_table = jnp.right_shift(packed_rows[:, :, None], shifts[None, None, :]) & 1
    bit_table = bit_table.reshape(packed_rows.shape[0], packed_rows.shape[1] * 16)
    column = jnp.arange(bit_table.shape[1], dtype=jnp.int32)
    return jnp.where(column[None, :] < valid_cols, bit_table, 0)


def mean_rows(packed, valid_cols, needed):
    total_rows = packed.shape[0]
    row_block = math.gcd(total_rows, 256)
    grouped = packed.reshape(total_rows // row_block, row_block, packed.shape[1])

    def one_block(row_piece):
        dense_rows = unpack_rows(row_piece, valid_cols)
        degree = jnp.sum(dense_rows, axis=1).astype(jnp.float32)
        summed = jnp.dot(
            dense_rows.astype(jnp.bfloat16), needed, preferred_element_type=jnp.float32
        )
        return (summed / jnp.maximum(degree, 1.0)[:, None]).astype(jnp.bfloat16)

    return lax.map(one_block, grouped).reshape(total_rows, needed.shape[1])


def pick_blocks(holding, wanted, arriving):
    inside = (wanted >= 0) & (wanted < arriving.shape[0])
    taken_rows = jnp.take(arriving, jnp.clip(wanted, 0, arriving.shape[0] - 1), axis=0)
    return jnp.where(inside[:, None], taken_rows, holding)


def per_device(
    features,
    self_weight1,
    neigh_weight1,
    need_first,
    count_first,
    adjacency_first,
    self_weight2,
    neigh_weight2,
    need_second,
    count_second,
    adjacency_second,
    seed_rows,
):
    batch_at = lax.axis_index("batch")
    rows_first = adjacency_first.shape[0]
    node_blocks = features.reshape(features.shape[0] // BLK, BLK * features.shape[1])
    wanted_first = need_first[0]
    empty_first = jnp.zeros((wanted_first.shape[0], node_blocks.shape[1]), jnp.bfloat16)
    fetched_first = pick_blocks(
        empty_first, wanted_first, lax.all_gather(node_blocks, "dom", axis=0, tiled=True)
    )
    needed_first = fetched_first.reshape(-1, features.shape[1])
    near_first = mean_rows(adjacency_first, count_first[0] * BLK, needed_first)
    self_first = lax.dynamic_slice_in_dim(features, batch_at * rows_first, rows_first, 0)
    weight_self, weight_near = (
        lax.all_gather(self_weight1, "batch", axis=1, tiled=True),
        lax.all_gather(neigh_weight1, "batch", axis=1, tiled=True),
    )
    partial_first = jnp.dot(self_first, weight_self, preferred_element_type=jnp.float32) + jnp.dot(
        near_first, weight_near, preferred_element_type=jnp.float32
    )
    summed_first = sent_and_summed(partial_first, "col", 1)
    hidden_first = jnp.maximum(summed_first, 0.0).astype(jnp.bfloat16)
    frontier = lax.all_gather(hidden_first, "batch", axis=0, tiled=True)
    front_blocks = frontier.reshape(frontier.shape[0] // BLK, BLK * frontier.shape[1])
    wanted_second = need_second[0]
    empty_second = jnp.zeros((wanted_second.shape[0], front_blocks.shape[1]), jnp.bfloat16)
    fetched_second = pick_blocks(
        empty_second, wanted_second, lax.all_gather(front_blocks, "dom", axis=0, tiled=True)
    )
    needed_second = fetched_second.reshape(-1, frontier.shape[1])
    near_second = mean_rows(adjacency_second, count_second[0] * BLK, needed_second)
    own_second = jnp.take(frontier, seed_rows, axis=0)
    weight_own, weight_far = (
        lax.all_gather(self_weight2, "batch", axis=1, tiled=True),
        lax.all_gather(neigh_weight2, "batch", axis=1, tiled=True),
    )
    partial_second = jnp.dot(own_second, weight_own, preferred_element_type=jnp.float32) + jnp.dot(
        near_second, weight_far, preferred_element_type=jnp.float32
    )
    return of_everyone(partial_second, "col")


def solution(mesh):
    placed = (
        P("dom", "col"),
        P("col", "batch"),
        P("col", "batch"),
        P(("dom", "batch"), None),
        P(("dom", "batch")),
        P(("dom", "batch"), None),
        P("col", "batch"),
        P("col", "batch"),
        P(("dom", "batch"), None),
        P(("dom", "batch")),
        P(("dom", "batch"), None),
        P(("dom", "batch")),
    )
    return jax.shard_map(
        per_device, mesh=mesh, in_specs=placed, out_specs=P(("dom", "batch"), None), check_vma=False
    )
```

profile of v0, /device:TPU:0, one launch (start us, length us, event | category | flops | bytes accessed | tf_op | source)
XLA Modules:
  0.0 310.1 jit_solution(4355814135532355377)
XLA Ops:
  9.7 4.6 %all_gather.21 = bf16[64,256]{1,0:T(8,128)(2,1)S(1)} all-gather(bf16[64,128]{1,0:T(8,128)(2,1)} %param.17), channel_id=1, replica_groups=mesh['dom'=32,'col'=2,'batch'=2] {'batch'}, dimensions={1}, use_global_device_ids=true | all-gather | bytes 49152 | tf_op jit(solution)/shard_map/all_gather | solution.py:87
  14.3 4.6 %all_gather.23 = bf16[64,256]{1,0:T(8,128)(2,1)S(1)} all-gather(bf16[64,128]{1,0:T(8,128)(2,1)} %param.18), channel_id=1, replica_groups=mesh['dom'=32,'col'=2,'batch'=2] {'batch'}, dimensions={1}, use_global_device_ids=true | all-gather | bytes 49152 | tf_op jit(solution)/shard_map/all_gather | solution.py:88
  23.4 41.6 %all-gather.5.cloned.1.call-done = bf16[512,8192]{1,0:T(8,128)(2,1)} async-done(((bf16[16,8192]{1,0:T(8,128)(2,1)}), bf16[512,8192]{1,0:T(8,128)(2,1)}) %all-gather.5.cloned.1.call-update) | async-done | bytes 8388624 | tf_op jit(solution)/shard_map/all_gather | solution.py:81
  65.0 6.6 %gather_fusion = bf16[64,8192]{1,0:T(8,128)(2,1)S(1)} fusion(bf16[512,8192]{1,0:T(8,128)(2,1)} %all-gather.5.cloned.1.call-done, s32[1024]{0:T(1024)S(1)} %pad_clamp_fusion.1), kind=kCustom, calls=%fused_computation | custom fusion | bytes 2097408 | tf_op jit(solution)/shard_map/jit(_take)/gather | solution.py:57
  71.6 3.3 %gather.17 = bf16[8192,64]{1,0:T(8,128)(2,1)} reshape(bf16[64,8192]{1,0:T(8,128)(2,1)S(1)} %gather_fusion) | data formatting | bytes 2097152 | tf_op jit(solution)/shard_map/jit(_take)/gather | solution.py:57
  74.9 7.0 %select_select_fusion.1 = bf16[8192,64]{1,0:T(8,128)(2,1)S(1)} fusion(bf16[8192,64]{1,0:T(8,128)(2,1)} %gather.17, pred[8192]{0:T(1024)(128)(4,1)S(1)} %get-tuple-element.101, pred[8192]{0:T(1024)(128)(4,1)S(1)} %get-tuple-element.102), kind=kLoop, calls=%fused_computation.30 | loop fusion | flops 1048576 | bytes 2113536 | tf_op jit(solution)/shard_map/jit(_where)/select_n | solution.py:58
  81.9 36.0 %while.20 = (s32[]{:T(128)}, bf16[4,256,64]{1,2,0:T(8,128)(2,1)S(1)}, s32[]{:T(128)}, s32[4,256,512]{2,1,0:T(8,128)}, bf16[8192,64]{1,0:T(8,128)(2,1)S(1)}, /*index=5*/s32[]{:T(128)}) while((s32[]{:T(128)}, bf16[4,256,64]{1,2,0:T(8,128)(2,1)S(1)}, s32[]{:T(128)}, s32[4,256,512]{2,1,0:T(8,128)}, bf16[8192,64]{1,0:T(8,128)(2,1)S(1)}, ...), condition=%wide.region_2.3_spmd, body=%wide.region_0.2_spmd.sunk | while | flops 285278464 | bytes 13832277 | solution.py:52
  86.2 3.6 %select_reduce_fusion.4 = s32[256]{0:T(256)S(1)} fusion(s32[256,512]{0,1:T(8,128)S(1)} %bitcast.97, pred[512,16]{1,0:T(8,128)(4,1)S(1)} %add_compare_fusion.4), kind=kLoop, calls=%fused_computation.7.clone.1 | loop fusion | flops 8388352 | bytes 533504 | tf_op jit(solution)/shard_map/while/body/eval_jaxpr/reduce_sum | solution.py:46
  95.2 3.6 %select_reduce_fusion.4 = s32[256]{0:T(256)S(1)} fusion(s32[256,512]{0,1:T(8,128)S(1)} %bitcast.97, pred[512,16]{1,0:T(8,128)(4,1)S(1)} %add_compare_fusion.4), kind=kLoop, calls=%fused_computation.7.clone.1 | loop fusion | flops 8388352 | bytes 533504 | tf_op jit(solution)/shard_map/while/body/eval_jaxpr/reduce_sum | solution.py:46
  104.2 3.6 %select_reduce_fusion.4 = s32[256]{0:T(256)S(1)} fusion(s32[256,512]{0,1:T(8,128)S(1)} %bitcast.97, pred[512,16]{1,0:T(8,128)(4,1)S(1)} %add_compare_fusion.4), kind=kLoop, calls=%fused_computation.7.clone.1 | loop fusion | flops 8388352 | bytes 533504 | tf_op jit(solution)/shard_map/while/body/eval_jaxpr/reduce_sum | solution.py:46
  113.2 3.6 %select_reduce_fusion.4 = s32[256]{0:T(256)S(1)} fusion(s32[256,512]{0,1:T(8,128)S(1)} %bitcast.97, pred[512,16]{1,0:T(8,128)(4,1)S(1)} %add_compare_fusion.4), kind=kLoop, calls=%fused_computation.7.clone.1 | loop fusion | flops 8388352 | bytes 533504 | tf_op jit(solution)/shard_map/while/body/eval_jaxpr/reduce_sum | solution.py:46
  119.5 19.6 %all_to_all.10 = f32[2,1024,128]{1,2,0:T(8,128)S(1)} all-to-all(f32[2,1024,128]{1,2,0:T(8,128)S(1)} %bitcast.100), channel_id=1, replica_groups=mesh['dom'=32,'col'=2,'batch'=2] {'col'}, dimensions={0} | all-to-all | bytes 2097152 | tf_op jit(solution)/shard_map/all_to_all | solution.py:18
  139.4 8.0 %all_gather.24 = bf16[2048,128]{1,0:T(8,128)(2,1)S(1)} all-gather(bf16[1024,128]{1,0:T(8,128)(2,1)S(1)} %maximum_convert_fusion), channel_id=1, replica_groups=mesh['dom'=32,'col'=2,'batch'=2] {'batch'}, dimensions={0}, use_global_device_ids=true | all-gather | bytes 786432 | tf_op jit(solution)/shard_map/all_gather | solution.py:95
  149.1 4.5 %all-gather = bf16[2,86,128]{2,1,0:T(8,128)(2,1)S(1)} all-gather(bf16[1,86,128]{2,1,0:T(8,128)(2,1)S(1)} %bitcast.106), channel_id=1, replica_groups=mesh['dom'=32,'col'=2,'batch'=2] {'batch'}, dimensions={0}, use_global_device_ids=true | all-gather | bytes 66048 | tf_op jit(solution)/shard_map/all_gather | solution.py:106
  153.6 4.7 %all-gather.1 = bf16[2,86,128]{2,1,0:T(8,128)(2,1)S(1)} all-gather(bf16[1,86,128]{2,1,0:T(8,128)(2,1)S(1)} %bitcast.107), channel_id=1, replica_groups=mesh['dom'=32,'col'=2,'batch'=2] {'batch'}, dimensions={0}, use_global_device_ids=true | all-gather | bytes 66048 | tf_op jit(solution)/shard_map/all_gather | solution.py:107
  162.1 56.3 %all-gather.7.cloned.1.call-done = bf16[512,16384]{1,0:T(8,128)(2,1)} async-done(((bf16[16,16384]{1,0:T(8,128)(2,1)}), bf16[512,16384]{1,0:T(8,128)(2,1)}) %all-gather.7.cloned.1.call-update) | async-done | bytes 16777232 | tf_op jit(solution)/shard_map/all_gather | solution.py:100
  218.3 12.9 %gather_fusion.2 = bf16[64,16384]{1,0:T(8,128)(2,1)} fusion(bf16[512,16384]{1,0:T(8,128)(2,1)} %all-gather.7.cloned.1.call-done, s32[1024]{0:T(1024)S(1)} %pad_clamp_fusion), kind=kCustom, calls=%fused_computation.2 | custom fusion | bytes 4194560 | tf_op jit(solution)/shard_map/jit(_take)/gather | solution.py:57
  234.2 6.7 %select_select_fusion = bf16[8192,128]{1,0:T(8,128)(2,1)} fusion(bf16[8192,128]{1,0:T(8,128)(2,1)S(1)} %gather.20, pred[8192]{0:T(1024)(128)(4,1)S(1)} %get-tuple-element.103, pred[8192]{0:T(1024)(128)(4,1)S(1)} %get-tuple-element.104), kind=kLoop, calls=%fused_computation.29 | loop fusion | flops 2097152 | bytes 4210688 | tf_op jit(solution)/shard_map/jit(_where)/select_n | solution.py:58
  240.9 37.2 %while.21 = (s32[]{:T(128)}, bf16[4,256,128]{2,1,0:T(8,128)(2,1)S(1)}, s32[]{:T(128)}, s32[4,256,512]{2,1,0:T(8,128)}, bf16[8192,128]{1,0:T(8,128)(2,1)}, /*index=5*/s32[]{:T(128)}) while((s32[]{:T(128)}, bf16[4,256,128]{2,1,0:T(8,128)(2,1)S(1)}, s32[]{:T(128)}, s32[4,256,512]{2,1,0:T(8,128)}, bf16[8192,128]{1,0:T(8,128)(2,1)}, ...), condition=%wide.region_6.7_spmd, body=%wide.region_4.6_spmd.sunk | while | flops 553746688 | bytes 22253680 | solution.py:52
  245.2 3.6 %select_reduce_fusion.5 = s32[256]{0:T(256)S(1)} fusion(s32[256,512]{0,1:T(8,128)S(1)} %bitcast.99, pred[512,16]{1,0:T(8,128)(4,1)S(1)} %add_compare_fusion.5), kind=kLoop, calls=%fused_computation.20.clone.1 | loop fusion | flops 8388352 | bytes 533504 | tf_op jit(solution)/shard_map/while/body/eval_jaxpr/reduce_sum | solution.py:46
  254.5 3.6 %select_reduce_fusion.5 = s32[256]{0:T(256)S(1)} fusion(s32[256,512]{0,1:T(8,128)S(1)} %bitcast.99, pred[512,16]{1,0:T(8,128)(4,1)S(1)} %add_compare_fusion.5), kind=kLoop, calls=%fused_computation.20.clone.1 | loop fusion | flops 8388352 | bytes 533504 | tf_op jit(solution)/shard_map/while/body/eval_jaxpr/reduce_sum | solution.py:46
  263.8 3.6 %select_reduce_fusion.5 = s32[256]{0:T(256)S(1)} fusion(s32[256,512]{0,1:T(8,128)S(1)} %bitcast.99, pred[512,16]{1,0:T(8,128)(4,1)S(1)} %add_compare_fusion.5), kind=kLoop, calls=%fused_computation.20.clone.1 | loop fusion | flops 8388352 | bytes 533504 | tf_op jit(solution)/shard_map/while/body/eval_jaxpr/reduce_sum | solution.py:46
  273.1 3.6 %select_reduce_fusion.5 = s32[256]{0:T(256)S(1)} fusion(s32[256,512]{0,1:T(8,128)S(1)} %bitcast.99, pred[512,16]{1,0:T(8,128)(4,1)S(1)} %add_compare_fusion.5), kind=kLoop, calls=%fused_computation.20.clone.1 | loop fusion | flops 8388352 | bytes 533504 | tf_op jit(solution)/shard_map/while/body/eval_jaxpr/reduce_sum | solution.py:46
  278.5 23.8 %all_to_all.11 = f32[2,1024,172]{1,2,0:T(8,128)S(1)} all-to-all(f32[2,1024,172]{1,2,0:T(8,128)S(1)} %broadcast_in_dim.146), channel_id=1, replica_groups=mesh['dom'=32,'col'=2,'batch'=2] {'col'}, dimensions={0} | all-to-all | bytes 2818048 | tf_op jit(solution)/shard_map/all_to_all | solution.py:24
  (123 shorter events, 61.6 us)
Async XLA Ops:
  6.5 58.5 %all-gather.5.cloned.1.call-start = ((), (), s32[]{:S(2)}) async-start(), calls=%async_computation.2 | async-start | bytes 8650752 | tf_op jit(solution)/shard_map/all_gather | solution.py:81
  9.0 209.4 %all-gather.7.cloned.1.call-start = ((), (), s32[]{:S(2)}) async-start(), calls=%async_computation.3 | async-start | bytes 17301504 | tf_op jit(solution)/shard_map/all_gather | solution.py:100
  117.9 31.2 %copy-start.1 = (bf16[128,86]{0,1:T(8,128)(2,1)S(1)}, bf16[128,86]{0,1:T(8,128)(2,1)}, u32[]{:S(2)}) copy-start(bf16[128,86]{0,1:T(8,128)(2,1)} %param.22) | copy-start | bytes 66052
  117.9 35.7 %copy-start.2 = (bf16[128,86]{0,1:T(8,128)(2,1)S(1)}, bf16[128,86]{0,1:T(8,128)(2,1)}, u32[]{:S(2)}) copy-start(bf16[128,86]{0,1:T(8,128)(2,1)} %param.23) | copy-start | bytes 66052
  117.9 40.3 %copy-start.4 = (s32[1,64]{1,0:T(1,128)S(1)}, s32[1,64]{1,0:T(1,128)}, u32[]{:S(2)}) copy-start(s32[1,64]{1,0:T(1,128)} %param.24) | copy-start | bytes 772
  117.9 40.4 %copy-start.3 = (s32[1024]{0:T(1024)S(1)}, s32[1024]{0:T(1024)}, u32[]{:S(2)}) copy-start(s32[1024]{0:T(1024)} %param.27) | copy-start | bytes 12292
  242.3 6.5 %copy-start = (bf16[8192,128]{1,0:T(8,128)(2,1)S(1)}, bf16[8192,128]{1,0:T(8,128)(2,1)}, u32[]{:S(2)}) copy-start(bf16[8192,128]{1,0:T(8,128)(2,1)} %get-tuple-element.201) | copy-start | bytes 6291460 | tf_op jit(solution)/shard_map/while
  251.6 6.5 %copy-start = (bf16[8192,128]{1,0:T(8,128)(2,1)S(1)}, bf16[8192,128]{1,0:T(8,128)(2,1)}, u32[]{:S(2)}) copy-start(bf16[8192,128]{1,0:T(8,128)(2,1)} %get-tuple-element.201) | copy-start | bytes 6291460 | tf_op jit(solution)/shard_map/while
  260.9 6.5 %copy-start = (bf16[8192,128]{1,0:T(8,128)(2,1)S(1)}, bf16[8192,128]{1,0:T(8,128)(2,1)}, u32[]{:S(2)}) copy-start(bf16[8192,128]{1,0:T(8,128)(2,1)} %get-tuple-element.201) | copy-start | bytes 6291460 | tf_op jit(solution)/shard_map/while
  270.3 6.5 %copy-start = (bf16[8192,128]{1,0:T(8,128)(2,1)S(1)}, bf16[8192,128]{1,0:T(8,128)(2,1)}, u32[]{:S(2)}) copy-start(bf16[8192,128]{1,0:T(8,128)(2,1)} %get-tuple-element.201) | copy-start | bytes 6291460 | tf_op jit(solution)/shard_map/while
Sparse Core Ops, SparseCore 0:
  9.6 55.3 all-gather.4
  148.5 69.7 all-gather.6
where the time goes:
time: 311 us; the launch traced here: 310 us
  waiting for transfers between devices  97.9 us (31%)
  blocking collectives  69.7 us (22%)
  other arithmetic  68.5 us (22%)
  local copies, waits for them, and re-layouts  44.3 us (14%)
  between operations  15 us (5%)
  matrix products  14 us (5%)
    all_gather x1, waiting for transfers between devices, per_device(): lax.all_gather(front_blocks, 'dom', axis=0, tiled=True)  56.3 us
    all_gather x1, waiting for transfers between devices, per_device(): lax.all_gather(node_blocks, 'dom', axis=0, tiled=True)  41.6 us
    reduce_sum x8, other arithmetic, one_block(): degree = jnp.sum(dense_rows, axis=1).astype(jnp.float32)  28.7 us
    gather x4, local copies, waits for them, and re-layouts, pick_blocks(): jnp.take(arriving, jnp.clip(wanted, 0, arriving.shape[0] - 1), axis=0)  25.7 us
    all_to_all x1, blocking collectives, from_everyone(): return lax.all_to_all(copies, axis, split_axis=0, concat_axis=0, tiled=True)  23.8 us
    convert_element_type x8, other arithmetic, one_block(): dense_rows.astype(jnp.bfloat16)  22.2 us
    all_to_all x1, blocking collectives, sent_and_summed(): lax.all_to_all(in_blocks(shard, dim, devices), axis, 0, 0, tiled=True)  19.6 us
    select_n x2, other arithmetic, pick_blocks(): return jnp.where(inside[:, None], taken_rows, holding)  13.7 us
  transfers between devices with their start and end apart: 2, of which 2 were waited for; matrix products, arithmetic and copies ran while one was open for 3% of the time, Pallas kernels for 0%

commit v1 on v0

--- a/solution.py
+++ b/solution.py
@@ -97,7 +97,11 @@
     wanted_second = need_second[0]
     empty_second = jnp.zeros((wanted_second.shape[0], front_blocks.shape[1]), jnp.bfloat16)
     fetched_second = pick_blocks(
-        empty_second, wanted_second, lax.all_gather(front_blocks, "dom", axis=0, tiled=True)
+        empty_second,
+        wanted_second,
+        jnp.concatenate(
+            lax.all_to_all(jnp.stack([front_blocks] * lax.axis_size("dom")), "dom", 0, 0), axis=0
+        ),
     )
     needed_second = fetched_second.reshape(-1, frontier.shape[1])
     near_second = mean_rows(adjacency_second, count_second[0] * BLK, needed_second)

time: 311 us -> 458 us (1.47)
  waiting for transfers between devices: 97.9 us -> 241 us
  blocking collectives: 69.7 us -> 61.5 us
  starting transfers between devices: 0.04 us -> 5.76 us
  local copies, waits for them, and re-layouts: 44.3 us -> 49.5 us
    all_to_all x0 -> x1, waiting for transfers between devices: none -> 200 us  [per_device(): lax.all_to_all(jnp.stack([front_blocks] * lax.axis_size('dom')), 'dom', 0...]
    all_gather x1 -> x0, waiting for transfers between devices: 56.3 us -> none  [per_device(): lax.all_gather(front_blocks, 'dom', axis=0, tiled=True)]
    all_to_all x1, blocking collectives: 23.8 us -> 15.5 us  [from_everyone(): return lax.all_to_all(copies, axis, split_axis=0, concat_axis=0, tiled=True)]
    another operation x0 -> x2, local copies, waits for them, and re-layouts: none -> 6.19 us  [per_device(): jnp.stack([front_blocks] * lax.axis_size('dom'))]
    all_to_all x0 -> x1, starting transfers between devices: none -> 5.76 us  [per_device(): lax.all_to_all(jnp.stack([front_blocks] * lax.axis_size('dom')), 'dom', 0...]
  transfers between devices with their start and end apart: 2 -> 2, of which waited for: 2 -> 2; matrix products, arithmetic and copies ran while one was open for 3% -> 2% of each run, Pallas kernels for 0% -> 0%
where the time goes in v1:
time: 458 us; the launch traced here: 456 us
  waiting for transfers between devices  241 us (53%)
  other arithmetic  68.5 us (15%)
  blocking collectives  61.5 us (13%)
  local copies, waits for them, and re-layouts  49.5 us (11%)
  between operations  14.9 us (3%)
  matrix products  14 us (3%)
  starting transfers between devices  5.76 us (1%)
    all_to_all x1, waiting for transfers between devices, per_device(): lax.all_to_all(jnp.stack([front_blocks] * lax.axis_size('dom')), 'dom', 0...  200 us
    all_gather x1, waiting for transfers between devices, per_device(): lax.all_gather(node_blocks, 'dom', axis=0, tiled=True)  41.7 us
    reduce_sum x8, other arithmetic, one_block(): degree = jnp.sum(dense_rows, axis=1).astype(jnp.float32)  28.7 us
    gather x4, local copies, waits for them, and re-layouts, pick_blocks(): jnp.take(arriving, jnp.clip(wanted, 0, arriving.shape[0] - 1), axis=0)  25.7 us
    convert_element_type x8, other arithmetic, one_block(): dense_rows.astype(jnp.bfloat16)  22.2 us
    all_to_all x1, blocking collectives, sent_and_summed(): lax.all_to_all(in_blocks(shard, dim, devices), axis, 0, 0, tiled=True)  19.6 us
    all_to_all x1, blocking collectives, from_everyone(): return lax.all_to_all(copies, axis, split_axis=0, concat_axis=0, tiled=True)  15.5 us
    select_n x2, other arithmetic, pick_blocks(): return jnp.where(inside[:, None], taken_rows, holding)  13.7 us
  transfers between devices with their start and end apart: 2, of which 2 were waited for; matrix products, arithmetic and copies ran while one was open for 2% of the time, Pallas kernels for 0%

profile of v1, /device:TPU:0, one launch (start us, length us, event | category | flops | bytes accessed | tf_op | source)
XLA Modules:
  0.0 456.1 jit_solution(9602624572398264947)
XLA Ops:
  9.6 4.6 %all_gather.18 = bf16[64,256]{1,0:T(8,128)(2,1)S(1)} all-gather(bf16[64,128]{1,0:T(8,128)(2,1)} %param.17), channel_id=1, replica_groups=mesh['dom'=32,'col'=2,'batch'=2] {'batch'}, dimensions={1}, use_global_device_ids=true | all-gather | bytes 49152 | tf_op jit(solution)/shard_map/all_gather | solution.py:87
  14.3 4.6 %all_gather.20 = bf16[64,256]{1,0:T(8,128)(2,1)S(1)} all-gather(bf16[64,128]{1,0:T(8,128)(2,1)} %param.18), channel_id=1, replica_groups=mesh['dom'=32,'col'=2,'batch'=2] {'batch'}, dimensions={1}, use_global_device_ids=true | all-gather | bytes 49152 | tf_op jit(solution)/shard_map/all_gather | solution.py:88
  23.3 41.7 %all-gather.4.cloned.1.call-done = bf16[512,8192]{1,0:T(8,128)(2,1)} async-done(((bf16[16,8192]{1,0:T(8,128)(2,1)}), bf16[512,8192]{1,0:T(8,128)(2,1)}) %all-gather.4.cloned.1.call-update) | async-done | bytes 8388624 | tf_op jit(solution)/shard_map/all_gather | solution.py:81
  65.0 6.6 %gather_fusion = bf16[64,8192]{1,0:T(8,128)(2,1)S(1)} fusion(bf16[512,8192]{1,0:T(8,128)(2,1)} %all-gather.4.cloned.1.call-done, s32[1024]{0:T(1024)S(1)} %pad_clamp_fusion.1), kind=kCustom, calls=%fused_computation | custom fusion | bytes 2097408 | tf_op jit(solution)/shard_map/jit(_take)/gather | solution.py:57
  74.9 7.0 %select_select_fusion.1 = bf16[8192,64]{1,0:T(8,128)(2,1)S(1)} fusion(bf16[8192,64]{1,0:T(8,128)(2,1)} %gather.17, pred[8192]{0:T(1024)(128)(4,1)S(1)} %get-tuple-element.101, pred[8192]{0:T(1024)(128)(4,1)S(1)} %get-tuple-element.102), kind=kLoop, calls=%fused_computation.30 | loop fusion | flops 1048576 | bytes 2113536 | tf_op jit(solution)/shard_map/jit(_where)/select_n | solution.py:58
  81.9 36.0 %while.20 = (s32[]{:T(128)}, bf16[4,256,64]{1,2,0:T(8,128)(2,1)S(1)}, s32[]{:T(128)}, s32[4,256,512]{2,1,0:T(8,128)}, bf16[8192,64]{1,0:T(8,128)(2,1)S(1)}, /*index=5*/s32[]{:T(128)}) while((s32[]{:T(128)}, bf16[4,256,64]{1,2,0:T(8,128)(2,1)S(1)}, s32[]{:T(128)}, s32[4,256,512]{2,1,0:T(8,128)}, bf16[8192,64]{1,0:T(8,128)(2,1)S(1)}, ...), condition=%wide.region_2.3_spmd, body=%wide.region_0.2_spmd.sunk | while | flops 285278464 | bytes 13832277 | solution.py:52
  86.3 3.6 select_reduce_fusion.4
  95.2 3.6 select_reduce_fusion.4
  104.2 3.6 select_reduce_fusion.4
  113.2 3.6 select_reduce_fusion.4
  119.5 19.6 %all_to_all.15 = f32[2,1024,128]{1,2,0:T(8,128)S(1)} all-to-all(f32[2,1024,128]{1,2,0:T(8,128)S(1)} %bitcast.101), channel_id=1, replica_groups=mesh['dom'=32,'col'=2,'batch'=2] {'col'}, dimensions={0} | all-to-all | bytes 2097152 | tf_op jit(solution)/shard_map/all_to_all | solution.py:18
  139.3 8.0 %all_gather.21 = bf16[2048,128]{1,0:T(8,128)(2,1)S(1)} all-gather(bf16[1024,128]{1,0:T(8,128)(2,1)S(1)} %maximum_convert_fusion), channel_id=1, replica_groups=mesh['dom'=32,'col'=2,'batch'=2] {'batch'}, dimensions={0}, use_global_device_ids=true | all-gather | bytes 786432 | tf_op jit(solution)/shard_map/all_gather | solution.py:95
  147.6 6.0 %stack.3 = bf16[32,16,16384]{2,1,0:T(8,128)(2,1)} broadcast(bf16[16,16384]{1,0:T(8,128)(2,1)S(1)} %stack_reshape.2), dimensions={1,2} | broadcast | bytes 17301504 | tf_op jit(solution)/shard_map/stack | solution.py:103
  153.5 5.8 %all-to-all-start.1 = ((bf16[32,16,16384]{2,1,0:T(8,128)(2,1)}), bf16[32,16,16384]{2,1,0:T(8,128)(2,1)}, u32[]{:S(2)}, u32[]{:S(2)}) async-start(bf16[32,16,16384]{2,1,0:T(8,128)(2,1)} %stack.3), calls=%async_computation.1 | async-start | bytes 33554432 | tf_op jit(solution)/shard_map/all_to_all | solution.py:103
  160.0 4.5 all-gather
  164.5 4.7 %all-gather.1 = bf16[2,86,128]{2,1,0:T(8,128)(2,1)S(1)} all-gather(bf16[1,86,128]{2,1,0:T(8,128)(2,1)S(1)} %bitcast.108), channel_id=1, replica_groups=mesh['dom'=32,'col'=2,'batch'=2] {'batch'}, dimensions={0}, use_global_device_ids=true | all-gather | bytes 66048 | tf_op jit(solution)/shard_map/all_gather | solution.py:111
  173.0 199.6 %all-to-all-done.1 = bf16[32,16,16384]{2,1,0:T(8,128)(2,1)} async-done(((bf16[32,16,16384]{2,1,0:T(8,128)(2,1)}), bf16[32,16,16384]{2,1,0:T(8,128)(2,1)}, u32[]{:S(2)}, u32[]{:S(2)}) %all-to-all-start.1) | async-done | bytes 16777248 | tf_op jit(solution)/shard_map/all_to_all | solution.py:103
  372.6 12.9 %gather_fusion.2 = bf16[64,16384]{1,0:T(8,128)(2,1)} fusion(bf16[512,16384]{1,0:T(8,128)(2,1)} %bitcast.24, s32[1024]{0:T(1024)S(1)} %pad_clamp_fusion), kind=kCustom, calls=%fused_computation.2 | custom fusion | bytes 4194560 | tf_op jit(solution)/shard_map/jit(_take)/gather | solution.py:57
  388.4 6.7 %select_select_fusion = bf16[8192,128]{1,0:T(8,128)(2,1)} fusion(bf16[8192,128]{1,0:T(8,128)(2,1)S(1)} %gather.20, pred[8192]{0:T(1024)(128)(4,1)S(1)} %get-tuple-element.103, pred[8192]{0:T(1024)(128)(4,1)S(1)} %get-tuple-element.104), kind=kLoop, calls=%fused_computation.29 | loop fusion | flops 2097152 | bytes 4210688 | tf_op jit(solution)/shard_map/jit(_where)/select_n | solution.py:58
  395.1 37.2 %while.21 = (s32[]{:T(128)}, bf16[4,256,128]{2,1,0:T(8,128)(2,1)S(1)}, s32[]{:T(128)}, s32[4,256,512]{2,1,0:T(8,128)}, bf16[8192,128]{1,0:T(8,128)(2,1)}, /*index=5*/s32[]{:T(128)}) while((s32[]{:T(128)}, bf16[4,256,128]{2,1,0:T(8,128)(2,1)S(1)}, s32[]{:T(128)}, s32[4,256,512]{2,1,0:T(8,128)}, bf16[8192,128]{1,0:T(8,128)(2,1)}, ...), condition=%wide.region_6.7_spmd, body=%wide.region_4.6_spmd.sunk | while | flops 553746688 | bytes 22253680 | solution.py:52
  399.4 3.6 select_reduce_fusion.5
  408.7 3.6 select_reduce_fusion.5
  418.0 3.6 select_reduce_fusion.5
  432.7 15.5 %all_to_all.16 = f32[2,1024,172]{1,2,0:T(8,128)S(1)} all-to-all(f32[2,1024,172]{1,2,0:T(8,128)S(1)} %broadcast_in_dim.146), channel_id=1, replica_groups=mesh['dom'=32,'col'=2,'batch'=2] {'col'}, dimensions={0} | all-to-all | bytes 2818048 | tf_op jit(solution)/shard_map/all_to_all | solution.py:24
  (123 shorter events, 67.6 us)
Async XLA Ops:
  6.5 58.5 %all-gather.4.cloned.1.call-start = ((), (), s32[]{:S(2)}) async-start(), calls=%async_computation.3 | async-start | bytes 8650752 | tf_op jit(solution)/shard_map/all_gather | solution.py:81
  153.5 6.4 %copy-start.1 = (bf16[128,86]{0,1:T(8,128)(2,1)S(1)}, bf16[128,86]{0,1:T(8,128)(2,1)}, u32[]{:S(2)}) copy-start(bf16[128,86]{0,1:T(8,128)(2,1)} %param.22) | copy-start | bytes 66052
  153.5 10.9 %copy-start.2 = (bf16[128,86]{0,1:T(8,128)(2,1)S(1)}, bf16[128,86]{0,1:T(8,128)(2,1)}, u32[]{:S(2)}) copy-start(bf16[128,86]{0,1:T(8,128)(2,1)} %param.23) | copy-start | bytes 66052
  153.5 15.6 %copy-start.4 = (s32[1,64]{1,0:T(1,128)S(1)}, s32[1,64]{1,0:T(1,128)}, u32[]{:S(2)}) copy-start(s32[1,64]{1,0:T(1,128)} %param.24) | copy-start | bytes 772
  153.5 15.7 %copy-start.3 = (s32[1024]{0:T(1024)S(1)}, s32[1024]{0:T(1024)}, u32[]{:S(2)}) copy-start(s32[1024]{0:T(1024)} %param.27) | copy-start | bytes 12292
  153.5 219.0 %all-to-all-start.1 = ((bf16[32,16,16384]{2,1,0:T(8,128)(2,1)}), bf16[32,16,16384]{2,1,0:T(8,128)(2,1)}, u32[]{:S(2)}, u32[]{:S(2)}) async-start(bf16[32,16,16384]{2,1,0:T(8,128)(2,1)} %stack.3), calls=%async_computation.1 | async-start | bytes 33554432 | tf_op jit(solution)/shard_map/all_to_all | solution.py:103
  396.6 6.5 %copy-start = (bf16[8192,128]{1,0:T(8,128)(2,1)S(1)}, bf16[8192,128]{1,0:T(8,128)(2,1)}, u32[]{:S(2)}) copy-start(bf16[8192,128]{1,0:T(8,128)(2,1)} %get-tuple-element.201) | copy-start | bytes 6291460 | tf_op jit(solution)/shard_map/while
  405.9 6.5 %copy-start = (bf16[8192,128]{1,0:T(8,128)(2,1)S(1)}, bf16[8192,128]{1,0:T(8,128)(2,1)}, u32[]{:S(2)}) copy-start(bf16[8192,128]{1,0:T(8,128)(2,1)} %get-tuple-element.201) | copy-start | bytes 6291460 | tf_op jit(solution)/shard_map/while
  415.2 6.5 %copy-start = (bf16[8192,128]{1,0:T(8,128)(2,1)S(1)}, bf16[8192,128]{1,0:T(8,128)(2,1)}, u32[]{:S(2)}) copy-start(bf16[8192,128]{1,0:T(8,128)(2,1)} %get-tuple-element.201) | copy-start | bytes 6291460 | tf_op jit(solution)/shard_map/while
  424.5 6.5 %copy-start = (bf16[8192,128]{1,0:T(8,128)(2,1)S(1)}, bf16[8192,128]{1,0:T(8,128)(2,1)}, u32[]{:S(2)}) copy-start(bf16[8192,128]{1,0:T(8,128)(2,1)} %get-tuple-element.201) | copy-start | bytes 6291460 | tf_op jit(solution)/shard_map/while
Sparse Core Ops, SparseCore 0:
  9.6 55.3 all-gather.3
